TPU v7x, 32 devices: a whole 2x2x4 slice. The times are simulated.
32 devices in a mesh: row: 8 (over y, x, core), col: 4 (over z).
Axes of the slice: x: 2, y: 2, z: 4, core: 2. Of those that a mesh axis runs over, the one named last changes fastest.
Arguments:
- state: float32 [2048, 4, 1024], P('row', 'col'), may hold values from -6 to 6
- coupling: bfloat16 [2048, 4, 1024], P('row', 'col'), may hold values from -2 to 2, as said below
- coupling_t: bfloat16 [2, 2048, 4, 1024], P(None, 'row', 'col'), may hold values from -2 to 2, as said below
- factor: float32 [4, 4, 256, 256], P(None, 'col', 'row'), may hold values from -0.3 to 1.3
- cofactor: float32 [4, 4, 256, 256], P(None, 'col', 'row'), may hold values from -0.3 to 1.3
- rates: float32 [4, 4, 256], P(None, 'col'), may hold values from 0.5 to 2
Outputs:
- updated_state: float32 [2048, 4, 1024], P('row', 'col')
Inputs may be any that keep to these rules, and one draw needn't show every extreme that they name: coupling and coupling_t hold the same matrix A; its blocks A(i, k) are zero unless k > i. coupling_t holds the transposed blocks of the A in coupling.
All inputs are finite; a program needn't handle non-finite values.
Results may differ from a plain program's by a relative error of at most 0.0003.
Values may be sent and summed in bfloat16 or wider, within the bound.
A program may use at most 64 MiB of HBM per device.

v0:
```python
import jax
import jax.numpy as jnp
from jax import lax
from jax.sharding import PartitionSpec as P

STEPS = 2
HIGHEST_PRECISION = lax.Precision.HIGHEST


def broadcast(block, axis, source):
    block = jnp.where(lax.axis_index(axis) == source, block, jnp.zeros_like(block))
    return lax.psum(block, axis)


def from_behind(block, axis, distance):
    devices = range(lax.axis_size(axis))
    route = [((i - distance) % len(devices), i) for i in devices]
    return lax.ppermute(block, axis, route)


def solve_block(residual, left_p, left_q, left_e, right_p, right_q, right_e):
    middle = jnp.dot(
        left_q, residual, precision=HIGHEST_PRECISION, preferred_element_type=jnp.float32
    )
    middle = jnp.dot(
        middle, right_q.T, precision=HIGHEST_PRECISION, preferred_element_type=jnp.float32
    )
    middle = middle / (left_e[:, None] + right_e[None, :])
    product = jnp.dot(
        left_p, middle, precision=HIGHEST_PRECISION, preferred_element_type=jnp.float32
    )
    return -jnp.dot(
        product, right_p.T, precision=HIGHEST_PRECISION, preferred_element_type=jnp.float32
    )


def pick_slot(stacked, slot_index):
    return lax.dynamic_index_in_dim(stacked, slot_index, 0, keepdims=False)


def on_device(state, coupling, coupling_t, factor, cofactor, rates):
    row_count = lax.axis_size("row")
    col_count = lax.axis_size("col")
    half_rows = row_count // 2
    order_blocks = 2 * row_count
    col_slots = order_blocks // col_count
    block_size = state.shape[0]
    row_index = lax.axis_index("row")
    col_index = lax.axis_index("col")
    blocks = jnp.transpose(state.reshape(block_size, col_slots, block_size), (1, 0, 2))
    full_p, full_q = (
        lax.all_gather(factor, "row", axis=2, tiled=True),
        lax.all_gather(cofactor, "row", axis=2, tiled=True),
    )
    right_ps = full_p.reshape(col_slots, block_size, block_size)
    right_qs = full_q.reshape(col_slots, block_size, block_size)
    right_es = rates.reshape(col_slots, block_size)
    own_slot = row_index // col_count
    picked = (
        pick_slot(right_ps, own_slot),
        pick_slot(right_qs, own_slot),
        pick_slot(right_es, own_slot),
    )
    left_p, left_q, left_e = (
        broadcast(picked[0], "col", row_index % col_count),
        broadcast(picked[1], "col", row_index % col_count),
        broadcast(picked[2], "col", row_index % col_count),
    )
    upper_row = coupling.reshape(block_size, col_slots * block_size)
    lower_pair = coupling_t.reshape(2, block_size, col_slots * block_size)
    my_columns = col_index + col_count * jnp.arange(col_slots, dtype=jnp.int32)
    upper_now = upper_row
    for wave_step in range(STEPS):
        antidiag = order_blocks - 1 - wave_step
        partner = antidiag - row_index
        owner_col = partner % col_count
        slot_here = partner // col_count
        usable = row_index <= partner
        residual = pick_slot(blocks, slot_here)
        solution = solve_block(
            residual,
            left_p,
            left_q,
            left_e,
            pick_slot(right_ps, slot_here),
            pick_slot(right_qs, slot_here),
            pick_slot(right_es, slot_here),
        )
        solution = jnp.where(usable, solution, 0.0)
        written = jnp.where(usable & (col_index == owner_col), solution, residual)
        blocks = lax.dynamic_update_index_in_dim(blocks, written, slot_here, 0)
        shared = broadcast(solution, "col", owner_col)
        mirror = antidiag - my_columns
        use_row = mirror <= my_columns
        sources = jnp.clip(jnp.where(use_row, mirror, my_columns), 0, row_count - 1)
        offered = jnp.where((sources == row_index)[:, None, None], shared[None], 0.0)
        fetched = lax.psum(offered, "row")
        partner_blocks = jnp.where(use_row[:, None, None], fetched, jnp.swapaxes(fetched, 1, 2))
        if wave_step > 0:
            upper_now = from_behind(upper_row, "col", (col_count - wave_step) % col_count)
        receiver = (row_index - wave_step - half_rows) % row_count
        send_slot = jnp.where(receiver + wave_step >= row_count, 1, 0)
        send_piece = pick_slot(lower_pair, send_slot)
        lower_now = from_behind(send_piece, "row", (half_rows - wave_step) % row_count)
        upper_view = upper_now.reshape(block_size, col_slots, block_size)
        rolled = jnp.where(
            (col_index + wave_step) // col_count == 1, jnp.roll(upper_view, -1, axis=1), upper_view
        )
        lower_view = lower_now.reshape(block_size, col_slots, block_size)
        left_terms = jnp.einsum(
            "aub,ubc->uac", rolled.astype(jnp.float32), partner_blocks, precision=HIGHEST_PRECISION
        )
        right_terms = jnp.einsum(
            "ab,buc->uac", shared, lower_view.astype(jnp.float32), precision=HIGHEST_PRECISION
        )
        targets = (row_index <= my_columns) & (row_index + my_columns < antidiag)
        blocks = blocks - jnp.where(targets[:, None, None], left_terms + right_terms, 0.0)
    return jnp.transpose(blocks, (1, 0, 2)).reshape(block_size, 1, col_slots * block_size)


def solution(mesh):
    return jax.shard_map(
        on_device,
        mesh=mesh,
        in_specs=(
            P("row", "col", None),
            P("row", "col", None),
            P(None, "row", "col", None),
            P(None, "col", "row", None),
            P(None, "col", "row", None),
            P(None, "col", None),
        ),
        out_specs=P("row", "col", None),
        check_vma=False,
    )
```

profile of v0, /device:TPU:0, one launch (start us, length us, event | category | flops | bytes accessed | tf_op | source)
XLA Modules:
  0.0 328.6 jit_solution(1007737203448546680)
XLA Ops:
  6.5 0.7 all-gather.3.cloned.1.call-update
  7.3 0.7 all-gather.5.cloned.1.call-update
  8.1 27.3 %all-gather.3.cloned.1.call-done = f32[4,1,256,256]{3,2,1,0:T(8,128)} async-done(((f32[4,1,32,256]{3,2,1,0:T(8,128)}), f32[4,1,256,256]{3,2,1,0:T(8,128)}) %all-gather.3.cloned.1.call-update) | async-done | bytes 1048592 | tf_op jit(solution)/shard_map/all_gather | solution.py:52
  35.4 1.7 select_bitcast_fusion.1
  37.0 23.6 %all-gather.5.cloned.1.call-done = f32[4,1,256,256]{3,2,1,0:T(8,128)} async-done(((f32[4,1,32,256]{3,2,1,0:T(8,128)}), f32[4,1,256,256]{3,2,1,0:T(8,128)}) %all-gather.5.cloned.1.call-update) | async-done | bytes 1048592 | tf_op jit(solution)/shard_map/all_gather | solution.py:53
  60.7 1.7 select_bitcast_fusion
  62.4 1.0 copy.19
  63.4 0.1 copy.51
  63.5 0.7 copy-done.15
  64.2 11.9 %psum.51 = f32[256]{0:T(256)S(1)} all-reduce(f32[256]{0:T(256)S(1)} %bitcast.106), channel_id=1, replica_groups=mesh['row'=8,'col'=4] {'col'}, use_global_device_ids=true, to_apply=%region_2.3 | all-reduce | flops 256 | bytes 2048 | tf_op jit(solution)/shard_map/psum | solution.py:12
  76.1 25.7 %all-reduce.15.cloned.1.call-done = (f32[256,256]{1,0:T(8,128)}, f32[256,256]{1,0:T(8,128)}) async-done(((f32[256,256]{1,0:T(8,128)}, f32[256,256]{1,0:T(8,128)}), (f32[256,256]{1,0:T(8,128)}, f32[256,256]{1,0:T(8,128)})) %all-reduce.15.cloned.1.call-update) | async-done | bytes 524304 | tf_op jit(solution)/shard_map/psum | solution.py:12
  101.8 1.4 fusion.24
  103.2 1.4 convolution_divide_fusion.1
  104.6 0.4 fusion.45
  105.0 1.5 bitcast_dynamic-update-slice_fusion.1
  106.5 0.8 broadcast_select_fusion.3
  107.4 1.1 dynamic-slice_bitcast_fusion
  108.5 1.5 collective-permute-start
  110.0 32.9 %all-reduce.7.cloned.1.call-done = f32[256,256]{0,1:T(8,128)} async-done(((f32[256,256]{0,1:T(8,128)}), f32[256,256]{0,1:T(8,128)}) %all-reduce.7.cloned.1.call-update) | async-done | bytes 262160 | tf_op jit(solution)/shard_map/psum | solution.py:12
  142.9 2.1 broadcast_select_fusion.1
  145.0 1.0 copy-done.12
  146.0 0.4 reshape_reshape.3
  146.4 0.2 slice.19
  146.6 0.3 slice.18
  146.9 0.7 copy.46
  147.7 0.2 copy.24
  147.9 54.7 %all-reduce.9.cloned.1.call-done = f32[4,256,256]{1,2,0:T(8,128)} async-done(((f32[4,256,256]{1,2,0:T(8,128)}), f32[4,256,256]{1,2,0:T(8,128)}) %all-reduce.9.cloned.1.call-update) | async-done | bytes 1048592 | tf_op jit(solution)/shard_map/psum | solution.py:97
  202.5 1.6 copy.23
  204.2 1.7 fusion.7
  206.0 0.6 fusion.4
  206.7 0.9 copy-done.11
  207.6 0.4 fusion.19
  208.0 1.4 convolution_divide_fusion
  209.4 0.4 fusion.46
  209.8 1.4 bitcast_dynamic-update-slice_fusion
  211.3 0.7 broadcast_select_fusion.2
  212.2 0.3 copy-done.13
  212.4 3.3 collective-permute-start.1
  215.7 36.9 %all-reduce.11.cloned.1.call-done = f32[256,256]{0,1:T(8,128)} async-done(((f32[256,256]{0,1:T(8,128)}), f32[256,256]{0,1:T(8,128)}) %all-reduce.11.cloned.1.call-update) | async-done | bytes 262160 | tf_op jit(solution)/shard_map/psum | solution.py:12
  252.6 2.1 broadcast_select_fusion
  254.8 0.8 copy-done.4
  255.5 0.6 slice.21
  256.2 1.3 copy.30
  257.5 0.6 convolution_bitcast_fusion
  258.1 54.2 %all-reduce.13.cloned.1.call-done = f32[4,256,256]{1,2,0:T(8,128)} async-done(((f32[4,256,256]{1,2,0:T(8,128)}), f32[4,256,256]{1,2,0:T(8,128)}) %all-reduce.13.cloned.1.call-update) | async-done | bytes 1048592 | tf_op jit(solution)/shard_map/psum | solution.py:97
  312.4 2.6 copy.29
  315.0 3.2 fusion.1
  318.2 3.6 %copy.32 = f32[256,1,1024]{2,1,0:T(1,128)} copy(f32[256,1,1024]{0,2,1:T(8,128)} %bitcast.98) | data formatting | bytes 2097152 | tf_op jit(solution)/shard_map/reshape | solution.py:118
  (53 shorter events, 0.7 us)
Async XLA Ops:
  6.5 55.9 %copy-start.9 = (f32[256,1,1024]{2,1,0:T(1,128)S(1)}, f32[256,1,1024]{2,1,0:T(1,128)}, u32[]{:S(2)}) copy-start(f32[256,1,1024]{2,1,0:T(1,128)} %param.6) | copy-start | bytes 3145732
  6.5 28.8 %all-gather.3.cloned.1.call-start = ((), (), s32[]{:S(2)}) async-start(), calls=%async_computation | async-start | bytes 1179648 | tf_op jit(solution)/shard_map/all_gather | solution.py:52
  7.3 53.4 %all-gather.5.cloned.1.call-start = ((), (), s32[]{:S(2)}) async-start(), calls=%async_computation.1 | async-start | bytes 1179648 | tf_op jit(solution)/shard_map/all_gather | solution.py:53
  8.0 93.8 %all-reduce.15.cloned.1.call-start = ((), (), s32[]{:S(2)}) async-start(), calls=%async_computation.6 | async-start | bytes 1048576 | tf_op jit(solution)/shard_map/psum | solution.py:12
  62.4 80.6 %all-reduce.7.cloned.1.call-start = ((), (), s32[]{:S(2)}) async-start(), calls=%async_computation.2 | async-start | bytes 524288 | tf_op jit(solution)/shard_map/psum | solution.py:12
  63.5 0.7 copy-start.15
  103.2 1.4 copy-start.5
  105.0 2.4 copy-start.10
  106.5 2.0 copy-start.2
  107.3 95.2 %all-reduce.9.cloned.1.call-start = ((), (), s32[]{:S(2)}) async-start(), calls=%async_computation.3 | async-start | bytes 2097152 | tf_op jit(solution)/shard_map/psum | solution.py:97
  108.5 39.2 %collective-permute-start = (bf16[256,1024]{1,0:T(8,128)(2,1)}, bf16[256,1024]{1,0:T(8,128)(2,1)S(1)}, u32[]{:S(2)}, u32[]{:S(2)}) collective-permute-start(bf16[256,1024]{1,0:T(8,128)(2,1)} %get-tuple-element.8), channel_id=1, source_target_pairs={{16,0},{20,4},{24,8},{28,12},{0,16},{4,20},{8,24},{12,28},{17,1},{... | collective-permute-start | bytes 1572872 | tf_op jit(solution)/shard_map/ppermute | solution.py:18
  145.0 1.0 copy-start.12
  145.0 107.6 %all-reduce.11.cloned.1.call-start = ((), (), s32[]{:S(2)}) async-start(), calls=%async_computation.4 | async-start | bytes 524288 | tf_op jit(solution)/shard_map/psum | solution.py:12
  202.5 1.7 copy-start
  204.2 1.8 copy-start.3
  204.2 1.8 copy-start.7
  206.6 1.0 copy-start.11
  208.0 1.4 copy-start.6
  209.8 2.3 copy-start.14
  211.3 1.1 copy-start.13
  212.0 100.3 %all-reduce.13.cloned.1.call-start = ((), (), s32[]{:S(2)}) async-start(), calls=%async_computation.5 | async-start | bytes 2097152 | tf_op jit(solution)/shard_map/psum | solution.py:97
  212.1 44.1 %collective-permute-start.2 = (bf16[256,1024]{1,0:T(8,128)(2,1)S(1)}, bf16[256,1024]{1,0:T(8,128)(2,1)}, u32[]{:S(2)}, u32[]{:S(2)}) collective-permute-start(bf16[256,1024]{1,0:T(8,128)(2,1)S(1)} %copy-done.14), channel_id=1, source_target_pairs={{20,0},{24,4},{28,8},{0,12},{4,16},{8,20},{12,24},{16,28},{21,1},{... | collective-permute-start | bytes 1572872 | tf_op jit(solution)/shard_map/ppermute | solution.py:18
  212.4 42.3 %collective-permute-start.1 = (bf16[256,1024]{1,0:T(8,128)(2,1)S(1)}, bf16[256,1024]{1,0:T(8,128)(2,1)S(1)}, u32[]{:S(2)}, u32[]{:S(2)}) collective-permute-start(bf16[256,1024]{1,0:T(8,128)(2,1)S(1)} %bitcast.105), channel_id=1, source_target_pairs={{1,0},{2,1},{3,2},{0,3},{5,4},{6,5},{7,6},{4,7},{9,8},{10,9},{11,1... | collective-permute-start | bytes 1572872 | tf_op jit(solution)/shard_map/ppermute | solution.py:18
  254.7 0.8 copy-start.4
  256.2 1.3 copy-start.8
  312.4 2.6 copy-start.1
Sparse Core Ops, SparseCore 0:
  9.2 26.0 all-gather.2
  37.3 23.3 all-gather.4
  63.1 38.7 all-reduce.14
  107.4 35.4 all-reduce.6
  145.9 56.5 all-reduce.8
  212.2 40.3 all-reduce.10
  255.7 56.5 all-reduce.12
where the time goes:
time: 329 us
  waiting for transfers between devices  257 us (78%)
  local copies, waits for them, and re-layouts  17.3 us (5%)
  matrix products  14.4 us (4%)
  between operations  14 us (4%)
  blocking collectives  11.9 us (4%)
  other arithmetic  9.03 us (3%)
  starting transfers between devices  5.04 us (2%)
    psum x2, waiting for transfers between devices, on_device(): fetched = lax.psum(offered, 'row')  109 us
    psum x3, waiting for transfers between devices, broadcast(): return lax.psum(block, axis)  95.5 us
    all_gather x1, waiting for transfers between devices, on_device(): lax.all_gather(factor, 'row', axis=2, tiled=True)  27.3 us
    all_gather x1, waiting for transfers between devices, on_device(): lax.all_gather(cofactor, 'row', axis=2, tiled=True)  23.6 us
    psum x1, blocking collectives, broadcast(): return lax.psum(block, axis)  11.9 us
  transfers between devices with their start and end apart: 10, of which 7 were waited for; matrix products, arithmetic and copies ran while one was open for 4% of the time, Pallas kernels for 0%

commit v1 on v0

--- a/solution.py
+++ b/solution.py
@@ -50,7 +50,7 @@
     blocks = jnp.transpose(state.reshape(block_size, col_slots, block_size), (1, 0, 2))
     full_p, full_q = (
         lax.all_gather(factor, "row", axis=2, tiled=True),
-        lax.all_gather(cofactor, "row", axis=2, tiled=True),
+        jnp.concatenate(lax.all_gather(cofactor, "row"), axis=2),
     )
     right_ps = full_p.reshape(col_slots, block_size, block_size)
     right_qs = full_q.reshape(col_slots, block_size, block_size)

time: 329 us -> 329 us (level)
    all_gather x1, waiting for transfers between devices: 27.3 us -> 23.2 us  [on_device(): lax.all_gather(factor, 'row', axis=2, tiled=True)]
    all_gather x1, waiting for transfers between devices: 23.6 us -> 27.3 us  [on_device(): lax.all_gather(cofactor, 'row')]
where the time goes in v1:
time: 329 us; the launch traced here: 328 us
  waiting for transfers between devices  256 us (78%)
  local copies, waits for them, and re-layouts  19.2 us (6%)
  between operations  14.1 us (4%)
  matrix products  13.4 us (4%)
  blocking collectives  11.9 us (4%)
  other arithmetic  8.09 us (2%)
  starting transfers between devices  5.04 us (2%)
    psum x2, waiting for transfers between devices, on_device(): fetched = lax.psum(offered, 'row')  109 us
    psum x3, waiting for transfers between devices, broadcast(): return lax.psum(block, axis)  95.5 us
    all_gather x1, waiting for transfers between devices, on_device(): lax.all_gather(cofactor, 'row')  27.3 us
    all_gather x1, waiting for transfers between devices, on_device(): lax.all_gather(factor, 'row', axis=2, tiled=True)  23.2 us
    psum x1, blocking collectives, broadcast(): return lax.psum(block, axis)  11.9 us
  transfers between devices with their start and end apart: 10, of which 7 were waited for; matrix products, arithmetic and copies ran while one was open for 4% of the time, Pallas kernels for 0%

profile of v1, /device:TPU:0, one launch (start us, length us, event | category | flops | bytes accessed | tf_op | source)
XLA Modules:
  0.0 328.1 jit_solution(14976392365234482496)
XLA Ops:
  6.5 0.7 all-gather.6.cloned.1.call-update
  7.3 0.7 all-gather.4.cloned.1.call-update
  8.1 27.3 %all-gather.6.cloned.1.call-done = f32[32,1,32,256]{3,2,1,0:T(8,128)} async-done(((f32[4,1,32,256]{3,2,1,0:T(8,128)}), f32[32,1,32,256]{3,2,1,0:T(8,128)}) %all-gather.6.cloned.1.call-update) | async-done | bytes 1048592 | tf_op jit(solution)/shard_map/all_gather | solution.py:53
  35.3 1.3 copy.50
  36.7 0.7 select_bitcast_fusion
  37.4 23.2 %all-gather.4.cloned.1.call-done = f32[4,1,256,256]{3,2,1,0:T(8,128)} async-done(((f32[4,1,32,256]{3,2,1,0:T(8,128)}), f32[4,1,256,256]{3,2,1,0:T(8,128)}) %all-gather.4.cloned.1.call-update) | async-done | bytes 1048592 | tf_op jit(solution)/shard_map/all_gather | solution.py:52
  60.7 1.7 select_bitcast_fusion.1
  62.4 1.0 copy.49
  63.5 0.7 copy-done.16
  64.2 11.9 %psum.51 = f32[256]{0:T(256)S(1)} all-reduce(f32[256]{0:T(256)S(1)} %bitcast.114), channel_id=1, replica_groups=mesh['row'=8,'col'=4] {'col'}, use_global_device_ids=true, to_apply=%region_2.3 | all-reduce | flops 256 | bytes 2048 | tf_op jit(solution)/shard_map/psum | solution.py:12
  76.1 25.7 %all-reduce.15.cloned.1.call-done = (f32[256,256]{1,0:T(8,128)}, f32[256,256]{1,0:T(8,128)}) async-done(((f32[256,256]{1,0:T(8,128)}, f32[256,256]{1,0:T(8,128)}), (f32[256,256]{1,0:T(8,128)}, f32[256,256]{1,0:T(8,128)})) %all-reduce.15.cloned.1.call-update) | async-done | bytes 524304 | tf_op jit(solution)/shard_map/psum | solution.py:12
  101.8 1.4 fusion.24
  103.2 0.4 convolution_divide_fusion.1
  103.6 0.5 copy-done.6
  104.1 0.4 fusion.45
  104.5 1.5 bitcast_dynamic-update-slice_fusion.1
  106.0 0.8 broadcast_select_fusion.3
  106.9 1.1 dynamic-slice_bitcast_fusion
  108.0 1.5 collective-permute-start
  109.5 32.9 %all-reduce.7.cloned.1.call-done = f32[256,256]{0,1:T(8,128)} async-done(((f32[256,256]{0,1:T(8,128)}), f32[256,256]{0,1:T(8,128)}) %all-reduce.7.cloned.1.call-update) | async-done | bytes 262160 | tf_op jit(solution)/shard_map/psum | solution.py:12
  142.4 2.1 broadcast_select_fusion.1
  144.5 1.0 copy-done.13
  145.5 0.4 reshape_reshape.7
  146.1 0.3 slice.18
  146.4 0.7 copy.77
  147.2 0.2 copy.55
  147.4 54.7 %all-reduce.9.cloned.1.call-done = f32[4,256,256]{1,2,0:T(8,128)} async-done(((f32[4,256,256]{1,2,0:T(8,128)}), f32[4,256,256]{1,2,0:T(8,128)}) %all-reduce.9.cloned.1.call-update) | async-done | bytes 1048592 | tf_op jit(solution)/shard_map/psum | solution.py:97
  202.0 1.6 copy.54
  203.7 1.7 fusion.7
  205.5 0.6 fusion.4
  206.2 0.9 copy-done.12
  207.1 0.4 fusion.19
  207.5 1.4 convolution_divide_fusion
  208.9 0.4 fusion.46
  209.3 1.4 bitcast_dynamic-update-slice_fusion
  210.8 0.7 broadcast_select_fusion.2
  211.7 0.3 copy-done.14
  211.9 3.3 collective-permute-start.1
  215.2 36.9 %all-reduce.11.cloned.1.call-done = f32[256,256]{0,1:T(8,128)} async-done(((f32[256,256]{0,1:T(8,128)}), f32[256,256]{0,1:T(8,128)}) %all-reduce.11.cloned.1.call-update) | async-done | bytes 262160 | tf_op jit(solution)/shard_map/psum | solution.py:12
  252.1 2.1 broadcast_select_fusion
  254.3 0.8 copy-done.4
  255.0 0.7 slice.21
  255.7 1.3 copy.61
  257.0 0.6 convolution_bitcast_fusion
  257.6 54.2 %all-reduce.13.cloned.1.call-done = f32[4,256,256]{1,2,0:T(8,128)} async-done(((f32[4,256,256]{1,2,0:T(8,128)}), f32[4,256,256]{1,2,0:T(8,128)}) %all-reduce.13.cloned.1.call-update) | async-done | bytes 1048592 | tf_op jit(solution)/shard_map/psum | solution.py:97
  311.8 2.6 copy.60
  314.5 3.2 fusion.1
  317.6 3.6 %copy.63 = f32[256,1,1024]{2,1,0:T(1,128)} copy(f32[256,1,1024]{0,2,1:T(8,128)} %bitcast.102) | data formatting | bytes 2097152 | tf_op jit(solution)/shard_map/reshape | solution.py:118
  (56 shorter events, 0.9 us)
Async XLA Ops:
  6.5 28.8 %all-gather.6.cloned.1.call-start = ((), (), s32[]{:S(2)}) async-start(), calls=%async_computation.5 | async-start | bytes 1179648 | tf_op jit(solution)/shard_map/all_gather | solution.py:53
  7.3 53.4 %all-gather.4.cloned.1.call-start = ((), (), s32[]{:S(2)}) async-start(), calls=%async_computation | async-start | bytes 1179648 | tf_op jit(solution)/shard_map/all_gather | solution.py:52
  8.0 93.8 %all-reduce.15.cloned.1.call-start = ((), (), s32[]{:S(2)}) async-start(), calls=%async_computation.6 | async-start | bytes 1048576 | tf_op jit(solution)/shard_map/psum | solution.py:12
  36.7 66.5 %copy-start.5 = (f32[4,1,8,32,256]{4,3,2,0,1:T(8,128)}, f32[4,1,8,32,256]{4,3,2,0,1:T(8,128)S(1)}, u32[]{:S(2)}) copy-start(f32[4,1,8,32,256]{4,3,2,0,1:T(8,128)S(1)} %copy.50) | copy-start | bytes 3145732
  36.7 25.8 %copy-start.10 = (f32[256,1,1024]{2,1,0:T(1,128)S(1)}, f32[256,1,1024]{2,1,0:T(1,128)}, u32[]{:S(2)}) copy-start(f32[256,1,1024]{2,1,0:T(1,128)} %param.6) | copy-start | bytes 3145732
  62.3 80.1 %all-reduce.7.cloned.1.call-start = ((), (), s32[]{:S(2)}) async-start(), calls=%async_computation.1 | async-start | bytes 524288 | tf_op jit(solution)/shard_map/psum | solution.py:12
  63.5 0.7 copy-start.16
  103.2 1.0 copy-start.6
  104.5 2.4 copy-start.11
  106.0 2.0 copy-start.2
  106.8 95.2 %all-reduce.9.cloned.1.call-start = ((), (), s32[]{:S(2)}) async-start(), calls=%async_computation.2 | async-start | bytes 2097152 | tf_op jit(solution)/shard_map/psum | solution.py:97
  108.0 39.2 %collective-permute-start = (bf16[256,1024]{1,0:T(8,128)(2,1)}, bf16[256,1024]{1,0:T(8,128)(2,1)S(1)}, u32[]{:S(2)}, u32[]{:S(2)}) collective-permute-start(bf16[256,1024]{1,0:T(8,128)(2,1)} %get-tuple-element.8), channel_id=1, source_target_pairs={{16,0},{20,4},{24,8},{28,12},{0,16},{4,20},{8,24},{12,28},{17,1},{... | collective-permute-start | bytes 1572872 | tf_op jit(solution)/shard_map/ppermute | solution.py:18
  144.5 1.0 copy-start.13
  144.5 107.6 %all-reduce.11.cloned.1.call-start = ((), (), s32[]{:S(2)}) async-start(), calls=%async_computation.3 | async-start | bytes 524288 | tf_op jit(solution)/shard_map/psum | solution.py:12
  202.0 1.7 copy-start
  203.7 1.8 copy-start.3
  203.7 1.8 copy-start.8
  206.1 1.0 copy-start.12
  207.5 1.4 copy-start.7
  209.3 2.3 copy-start.15
  210.8 1.1 copy-start.14
  211.5 100.3 %all-reduce.13.cloned.1.call-start = ((), (), s32[]{:S(2)}) async-start(), calls=%async_computation.4 | async-start | bytes 2097152 | tf_op jit(solution)/shard_map/psum | solution.py:97
  211.6 44.1 %collective-permute-start.2 = (bf16[256,1024]{1,0:T(8,128)(2,1)S(1)}, bf16[256,1024]{1,0:T(8,128)(2,1)}, u32[]{:S(2)}, u32[]{:S(2)}) collective-permute-start(bf16[256,1024]{1,0:T(8,128)(2,1)S(1)} %copy-done.15), channel_id=1, source_target_pairs={{20,0},{24,4},{28,8},{0,12},{4,16},{8,20},{12,24},{16,28},{21,1},{... | collective-permute-start | bytes 1572872 | tf_op jit(solution)/shard_map/ppermute | solution.py:18
  211.9 42.3 %collective-permute-start.1 = (bf16[256,1024]{1,0:T(8,128)(2,1)S(1)}, bf16[256,1024]{1,0:T(8,128)(2,1)S(1)}, u32[]{:S(2)}, u32[]{:S(2)}) collective-permute-start(bf16[256,1024]{1,0:T(8,128)(2,1)S(1)} %bitcast.113), channel_id=1, source_target_pairs={{1,0},{2,1},{3,2},{0,3},{5,4},{6,5},{7,6},{4,7},{9,8},{10,9},{11,1... | collective-permute-start | bytes 1572872 | tf_op jit(solution)/shard_map/ppermute | solution.py:18
  254.2 0.8 copy-start.4
  255.7 1.3 copy-start.9
  311.8 2.6 copy-start.1
Sparse Core Ops, SparseCore 0:
  9.2 26.0 all-gather.5
  37.2 23.3 all-gather.3
  63.0 38.7 all-reduce.14
  106.9 35.4 all-reduce.6
  145.4 56.5 all-reduce.8
  211.6 40.3 all-reduce.10
  255.2 56.5 all-reduce.12
